TPU v7x, 32 devices: a whole 2x2x4 slice. The times are simulated.
32 devices in a mesh: expert: 8 (over y, x, core), shard: 4 (over z).
Axes of the slice: x: 2, y: 2, z: 4, core: 2. Of those that a mesh axis runs over, the one named last changes fastest.
Arguments:
- w_gate: float32 [64, 2048, 1024], P('expert', 'shard'), may hold values from -0.1875 to 0.1875
- avg_gate: float32 [64, 2048, 1024], P('expert', 'shard'), may hold values from -0.125 to 0.125
- w_up: float32 [64, 2048, 1024], P('expert', 'shard'), may hold values from -0.1875 to 0.1875
- avg_up: float32 [64, 2048, 1024], P('expert', 'shard'), may hold values from -0.125 to 0.125
- mix_share: float32 [64], P('expert'), may hold values from 0.2 to 0.8
- router_weight: float32 [2048, 64], P('shard', 'expert'), may hold values from -0.125 to 0.125
- router_gain: float32 [2048], P('shard'), may hold values from 0.25 to 1.75
Outputs:
- serve_gate: bfloat16 [64, 2048, 1024], P('expert')
- serve_up: bfloat16 [64, 2048, 1024], P('expert')
- scale_gate: float32 [64, 1024], P('expert')
- scale_up: float32 [64, 1024], P('expert')
- serve_router: bfloat16 [2048, 64], replicated
All inputs are finite; a program needn't handle non-finite values.
Results may differ from a plain program's by a relative error of at most 0.001.
Values may be sent and summed in bfloat16 or wider, within the bound.
A program may use at most 256 MiB of HBM per device.

v0:
```python
import jax
import jax.numpy as jnp
from jax import lax
from jax.sharding import PartitionSpec as P


def per_device(w_gate, avg_gate, w_up, avg_up, mix_share, router_weight, router_gain):
    fresh_gate = mix_share[:, None, None] * w_gate + (1.0 - mix_share[:, None, None]) * avg_gate
    fresh_up = mix_share[:, None, None] * w_up + (1.0 - mix_share[:, None, None]) * avg_up
    total_gate, total_up = lax.psum(
        (jnp.sum(fresh_gate * fresh_gate, axis=1), jnp.sum(fresh_up * fresh_up, axis=1)), "shard"
    )
    scale_gate = jnp.sqrt(total_gate)
    scale_up = jnp.sqrt(total_up)
    narrow_gate, narrow_up = (
        (fresh_gate / jnp.expand_dims(scale_gate, 1)).astype(jnp.bfloat16),
        (fresh_up / jnp.expand_dims(scale_up, 1)).astype(jnp.bfloat16),
    )
    serve_gate, serve_up = (
        lax.all_gather(narrow_gate, "shard", axis=1, tiled=True),
        lax.all_gather(narrow_up, "shard", axis=1, tiled=True),
    )
    part_router = (router_weight * router_gain[:, None]).astype(jnp.bfloat16)
    row_router = lax.all_gather(part_router, "shard", axis=0, tiled=True)
    serve_router = lax.all_gather(row_router, "expert", axis=1, tiled=True)
    return (serve_gate, serve_up, scale_gate, scale_up, serve_router)


def solution(mesh):
    return jax.shard_map(
        per_device,
        mesh=mesh,
        in_specs=(
            P("expert", "shard", None),
            P("expert", "shard", None),
            P("expert", "shard", None),
            P("expert", "shard", None),
            P("expert"),
            P("shard", "expert"),
            P("shard"),
        ),
        out_specs=(
            P("expert", None, None),
            P("expert", None, None),
            P("expert", None),
            P("expert", None),
            P(),
        ),
        check_vma=False,
    )
```

profile of v0, /device:TPU:0, one launch (start us, length us, event | category | flops | bytes accessed | tf_op | source)
XLA Modules:
  0.0 1276.1 jit_solution(14333517205513151259)
XLA Ops:
  7.2 0.0 all-reduce.3.cloned.1.call-start
  7.2 0.7 broadcast_subtract_fusion
  7.9 0.0 copy-start.3
  7.9 23.3 %multiply_reduce_fusion = (f32[8,1024]{1,0:T(8,128)}, f32[8,1024]{1,0:T(8,128)}) fusion(f32[8,512,1024]{2,1,0:T(8,128)} %param.10, f32[8]{0:T(128)S(1)} %broadcast_subtract_fusion, f32[8,512,1024]{2,1,0:T(8,128)} %param.9, f32[8]{0:T(128)} %param.11, f32[8,512,1024]{2,1,0:T(8,128)} %param.8, f32[8,512,1024]{2,1,0:T(8,128)} %param.7), kind=kLoop, calls=%fused_computation.1 | loop fusion | flops 41926656 | bytes 67174464 | tf_op jit(solution)/shard_map/reduce_sum | solution.py:11
  31.1 0.0 all-reduce.3.cloned.1.call-update
  31.2 0.0 all-gather.3.cloned.1.call-start
  31.2 37.2 %all-reduce.3.cloned.1.call-done = (f32[8,1024]{1,0:T(8,128)}, f32[8,1024]{1,0:T(8,128)}) async-done(((f32[8,1024]{1,0:T(8,128)}, f32[8,1024]{1,0:T(8,128)}), (f32[8,1024]{1,0:T(8,128)}, f32[8,1024]{1,0:T(8,128)})) %all-reduce.3.cloned.1.call-update) | async-done | bytes 65552 | tf_op jit(solution)/shard_map/psum | solution.py:10
  68.4 0.8 sqrt.6
  69.2 0.0 copy-start
  69.2 0.8 sqrt.7
  70.0 0.0 copy-done.3
  70.0 0.0 copy-start.1
  70.0 29.3 %divide_convert_fusion = (bf16[8,512,1024]{2,1,0:T(8,128)(2,1)}, bf16[8,512,1024]{2,1,0:T(8,128)(2,1)}) fusion(f32[8,1024]{1,0:T(8,128)S(1)} %sqrt.7, f32[8,512,1024]{2,1,0:T(8,128)} %param.10, f32[8]{0:T(128)S(1)} %broadcast_subtract_fusion, f32[8,512,1024]{2,1,0:T(8,128)} %param.9, f32[8]{0:T(128)S(1)} %copy-done.3, f32[8,1024]{1,0:T(8,128)S(1)} %sqrt.6, ...), kind=kLoop, calls=%fused_computation | loop fusion | flops 41943040 | bytes 83951680 | tf_op jit(solution)/shard_map/convert_element_type | solution.py:17
  99.3 0.0 copy-done
  99.4 0.0 copy-done.1
  99.4 0.0 copy-start.2
  99.4 0.0 copy-start.4
  99.4 0.0 all-gather.3.cloned.1.call-update
  99.4 0.0 all-gather.5.cloned.1.call-start
  99.5 0.7 all-gather.5.cloned.1.call-update
  100.1 0.0 copy-done.2
  100.2 0.0 copy-done.4
  100.2 13.1 %all_gather.14 = bf16[2048,8]{0,1:T(8,128)(2,1)S(1)} all-gather(bf16[512,8]{0,1:T(8,128)(2,1)S(1)} %multiply_convert_fusion), channel_id=1, replica_groups=mesh['expert'=8,'shard'=4] {'shard'}, dimensions={0}, use_global_device_ids=true | all-gather | bytes 40960 | tf_op jit(solution)/shard_map/all_gather | solution.py:24
  113.3 9.2 all_gather.15
  122.6 538.1 %all-gather.3.cloned.1.call-done = bf16[8,2048,1024]{2,1,0:T(8,128)(2,1)} async-done(((bf16[8,512,1024]{2,1,0:T(8,128)(2,1)}), bf16[8,2048,1024]{2,1,0:T(8,128)(2,1)}) %all-gather.3.cloned.1.call-update) | async-done | bytes 33554448 | tf_op jit(solution)/shard_map/all_gather | solution.py:20
  660.7 561.8 %all-gather.5.cloned.1.call-done = bf16[8,2048,1024]{2,1,0:T(8,128)(2,1)} async-done(((bf16[8,512,1024]{2,1,0:T(8,128)(2,1)}), bf16[8,2048,1024]{2,1,0:T(8,128)(2,1)}) %all-gather.5.cloned.1.call-update) | async-done | bytes 33554448 | tf_op jit(solution)/shard_map/all_gather | solution.py:21
  1222.4 23.2 %copy.17 = bf16[8,2048,1024]{2,1,0:T(8,128)(2,1)} copy(bf16[8,2048,1024]{2,1,0:T(8,128)(2,1)} %all-gather.3.cloned.1.call-done) | data formatting | bytes 67108864
  1245.7 23.2 %copy.18 = bf16[8,2048,1024]{2,1,0:T(8,128)(2,1)} copy(bf16[8,2048,1024]{2,1,0:T(8,128)(2,1)} %all-gather.5.cloned.1.call-done) | data formatting | bytes 67108864
  1268.9 0.7 copy.19
  (1 shorter events, 0.0 us)
Async XLA Ops:
  7.2 61.2 %all-reduce.3.cloned.1.call-start = ((), (), s32[]{:S(2)}) async-start(), calls=%async_computation.2 | async-start | bytes 131072 | tf_op jit(solution)/shard_map/psum | solution.py:10
  7.9 62.1 %copy-start.3 = (f32[8]{0:T(128)S(1)}, f32[8]{0:T(128)}, u32[]{:S(2)}) copy-start(f32[8]{0:T(128)} %param.11) | copy-start | bytes 100
  31.2 629.5 %all-gather.3.cloned.1.call-start = ((), (), s32[]{:S(2)}) async-start(), calls=%async_computation | async-start | bytes 41943040 | tf_op jit(solution)/shard_map/all_gather | solution.py:20
  69.2 30.2 %copy-start = (f32[8,1024]{1,0:T(8,128)}, f32[8,1024]{1,0:T(8,128)S(1)}, u32[]{:S(2)}) copy-start(f32[8,1024]{1,0:T(8,128)S(1)} %sqrt.6) | copy-start | bytes 98308
  70.0 29.4 %copy-start.1 = (f32[8,1024]{1,0:T(8,128)}, f32[8,1024]{1,0:T(8,128)S(1)}, u32[]{:S(2)}) copy-start(f32[8,1024]{1,0:T(8,128)S(1)} %sqrt.7) | copy-start | bytes 98308
  99.4 0.8 copy-start.2
  99.4 0.8 copy-start.4
  99.4 1123.0 %all-gather.5.cloned.1.call-start = ((), (), s32[]{:S(2)}) async-start(), calls=%async_computation.1 | async-start | bytes 41943040 | tf_op jit(solution)/shard_map/all_gather | solution.py:21
Sparse Core Ops, SparseCore 0:
  31.3 37.0 all-reduce.2
  99.5 561.0 all-gather.2
  662.8 559.5 all-gather.4
where the time goes:
time: 1280 us
  waiting for transfers between devices  1140 us (89%)
  other arithmetic  53.3 us (4%)
  local copies, waits for them, and re-layouts  48.7 us (4%)
  blocking collectives  22.4 us (2%)
  between operations  13.8 us (1%)
    all_gather x1, waiting for transfers between devices, per_device(): lax.all_gather(narrow_up, 'shard', axis=1, tiled=True)  562 us
    all_gather x1, waiting for transfers between devices, per_device(): lax.all_gather(narrow_gate, 'shard', axis=1, tiled=True)  538 us
    unnamed x13, local copies, waits for them, and re-layouts  47.2 us
    psum x1, waiting for transfers between devices, per_device(): lax.psum((jnp.sum(fresh_gate * fresh_gate, axis=1), jnp.sum(fresh_up * fr...  37.2 us
    convert_element_type x1, other arithmetic, per_device(): (fresh_up / jnp.expand_dims(scale_up, 1)).astype(jnp.bfloat16)  29.3 us
  transfers between devices with their start and end apart: 3, of which 3 were waited for; matrix products, arithmetic and copies ran while one was open for 0% of the time, Pallas kernels for 0%

commit v1 on v0

v1 whole, which is shorter than its diff:
```python
import functools

import jax
import jax.numpy as jnp
from jax import lax
from jax.experimental import pallas as pl
from jax.experimental.pallas import tpu as pltpu
from jax.sharding import PartitionSpec as P

MESH = pl.DeviceIdType.MESH
SLOTS = 4
ROWS = 16


def kernel(
    ns, experts, rows, mix_ref, wg_ref, ag_ref, wu_ref, au_ref,
    og_ref, ou_ref, sg_ref, su_ref,
    fresh, other, narrow, head, tail,
    w_sem, a_sem, local_sem, recv_sem, right_sem, left_sem, head_send, head_recv, tail_send, tail_recv,
):
    z = lax.axis_index("shard")
    n = 2 * experts
    firsts, seconds, outs, scales = (wg_ref, wu_ref), (ag_ref, au_ref), (og_ref, ou_ref), (sg_ref, su_ref)

    barrier = pltpu.get_barrier_semaphore()
    for k in range(1, ns):
        pl.semaphore_signal(barrier, inc=1, device_id={"shard": lax.rem(z + k, ns)}, device_id_type=MESH)

    def w_copy(e, which):
        c = 2 * e + which
        return pltpu.make_async_copy(firsts[which].at[e], fresh.at[c], w_sem.at[c])

    def a_copy(e, which):
        slot = lax.rem(2 * e + which, SLOTS)
        return pltpu.make_async_copy(seconds[which].at[e], other.at[slot], a_sem.at[slot])

    def place(e, which, j):
        return outs[which].at[e, pl.ds(pl.multiple_of(j * rows, rows), rows), :]

    def local_copy(e, which):
        c = 2 * e + which
        return pltpu.make_async_copy(narrow.at[c], place(e, which, z), local_sem.at[c])

    def to_right(e, which, d):
        c = 2 * e + which
        src = narrow.at[c] if d == 0 else place(e, which, z - d)
        return pltpu.make_async_remote_copy(
            src_ref=src, dst_ref=place(e, which, z - d), send_sem=right_sem.at[d, c],
            recv_sem=recv_sem.at[z - d, c], device_id={"shard": z + 1}, device_id_type=MESH,
        )

    def to_left(e, which, d):
        c = 2 * e + which
        src = narrow.at[c] if d == 0 else place(e, which, z + d)
        return pltpu.make_async_remote_copy(
            src_ref=src, dst_ref=place(e, which, z + d), send_sem=left_sem.at[d, c],
            recv_sem=recv_sem.at[z + d, c], device_id={"shard": z - 1}, device_id_type=MESH,
        )

    def arrival(e, which, j):
        c = 2 * e + which
        return pltpu.make_async_copy(place(e, which, j), place(e, which, j), recv_sem.at[j, c])

    def sums_to(part, send, recv, k):
        return pltpu.make_async_remote_copy(
            src_ref=part.at[z], dst_ref=part.at[z], send_sem=send.at[k], recv_sem=recv.at[z],
            device_id={"shard": lax.rem(z + k, ns)}, device_id_type=MESH,
        )

    def sums_from(part, recv, k):
        j = lax.rem(z + k, ns)
        return pltpu.make_async_copy(part.at[j], part.at[j], recv.at[j])

    def mix(e, which, part, row):
        c = 2 * e + which
        slot = lax.rem(c, SLOTS)
        w_copy(e, which).wait()
        a_copy(e, which).wait()
        share = mix_ref[e]
        rest = 1.0 - share

        def step(i, acc):
            r = pl.ds(pl.multiple_of(i * ROWS, ROWS), ROWS)
            value = share * fresh[c, r, :] + rest * other[slot, r, :]
            fresh[c, r, :] = value
            square = value * value
            for k in range(0, ROWS, 8):
                acc = acc + square[k : k + 8]
            return acc

        acc = lax.fori_loop(0, rows // ROWS, step, jnp.zeros((8, fresh.shape[2]), jnp.float32), unroll=2)
        part[z, pl.ds(row, 1), :] = jnp.sum(acc, axis=0, keepdims=True)

    def finish(e, which, part, row):
        c = 2 * e + which
        total = part[0, pl.ds(row, 1), :]
        for j in range(1, ns):
            total = total + part[j, pl.ds(row, 1), :]
        scale = jnp.sqrt(total)
        scales[which][pl.ds(e, 1), :] = scale
        wide = jnp.broadcast_to(scale, (8, scale.shape[1]))
        wide = jnp.concatenate([wide] * (ROWS // 8), axis=0)

        def step(i, carry):
            r = pl.ds(pl.multiple_of(i * ROWS, ROWS), ROWS)
            narrow[c, r, :] = (fresh[c, r, :] / wide).astype(jnp.bfloat16)
            return carry

        lax.fori_loop(0, rows // ROWS, step, 0, unroll=2)

        @pl.when(z < ns - 1)
        def _():
            to_right(e, which, 0).start()

        @pl.when(z > 0)
        def _():
            to_left(e, which, 0).start()

        local_copy(e, which).start()

    for c in range(min(SLOTS, n)):
        w_copy(c // 2, c % 2).start()
        a_copy(c // 2, c % 2).start()
    for c in range(SLOTS, n):
        w_copy(c // 2, c % 2).start()

    def refill(e, which):
        if experts > SLOTS // 2:
            @pl.when(e + SLOTS // 2 < experts)
            def _():
                a_copy(e + SLOTS // 2, which).start()

    mix(0, 0, head, 0)
    refill(0, 0)
    mix(0, 1, head, 1)
    refill(0, 1)
    pl.semaphore_wait(barrier, ns - 1)
    for k in range(1, ns):
        sums_to(head, head_send, head_recv, k).start()
    if experts > 1:
        mix(1, 0, tail, 0)
        refill(1, 0)
    for k in range(1, ns):
        sums_from(head, head_recv, k).wait()
    finish(0, 0, head, 0)
    if experts > 1:
        mix(1, 1, tail, 1)
        refill(1, 1)

        def more(e, carry):
            for which in range(2):
                mix(e, which, tail, 2 * (e - 1) + which)
                refill(e, which)
            return carry

        lax.fori_loop(2, experts, more, 0)
        for k in range(1, ns):
            sums_to(tail, tail_send, tail_recv, k).start()
    finish(0, 1, head, 1)
    if experts > 1:
        for k in range(1, ns):
            sums_from(tail, tail_recv, k).wait()

        def rest(e, carry):
            for which in range(2):
                finish(e, which, tail, 2 * (e - 1) + which)
            return carry

        lax.fori_loop(1, experts, rest, 0)

    for d in range(1, ns):
        def pass_on(e, carry, d=d):
            for which in range(2):
                @pl.when(z >= d)
                def _():
                    arrival(e, which, z - d).wait()

                @pl.when(z + d < ns)
                def _():
                    arrival(e, which, z + d).wait()

                if d < ns - 1:
                    @pl.when((z >= d) & (z < ns - 1))
                    def _():
                        to_right(e, which, d).start()

                    @pl.when((z + d < ns) & (z > 0))
                    def _():
                        to_left(e, which, d).start()
            return carry

        lax.fori_loop(0, experts, pass_on, 0)

    def drain(e, carry):
        for which in range(2):
            local_copy(e, which).wait()
            for d in range(ns - 1):
                @pl.when((z >= d) & (z < ns - 1))
                def _():
                    to_right(e, which, d).wait_send()

                @pl.when((z + d < ns) & (z > 0))
                def _():
                    to_left(e, which, d).wait_send()
        return carry

    lax.fori_loop(0, experts, drain, 0)
    for k in range(1, ns):
        sums_to(head, head_send, head_recv, k).wait_send()
        if experts > 1:
            sums_to(tail, tail_send, tail_recv, k).wait_send()


def solution(mesh):
    ns, ne = mesh.shape["shard"], mesh.shape["expert"]

    def per_device(w_gate, avg_gate, w_up, avg_up, mix_share, router_weight, router_gain):
        experts, rows, cols = w_gate.shape
        n = 2 * experts
        dma = pltpu.SemaphoreType.DMA
        anywhere = pl.BlockSpec(memory_space=pl.ANY)
        vmem = pl.BlockSpec(memory_space=pltpu.VMEM)
        serve = jax.ShapeDtypeStruct((experts, ns * rows, cols), jnp.bfloat16)
        scale = jax.ShapeDtypeStruct((experts, cols), jnp.float32)

        part_router = (router_weight * router_gain[:, None]).astype(jnp.bfloat16).T
        every = lax.all_gather(part_router, ("shard", "expert"), axis=0, tiled=False)
        every = every.reshape(ns, ne, part_router.shape[0], rows)
        serve_router = every.transpose(0, 3, 1, 2).reshape(ns * rows, ne * part_router.shape[0])

        serve_gate, serve_up, scale_gate, scale_up = pl.pallas_call(
            functools.partial(kernel, ns, experts, rows),
            out_shape=(serve, serve, scale, scale),
            in_specs=[pl.BlockSpec(memory_space=pltpu.SMEM)] + [anywhere] * 4,
            out_specs=(anywhere, anywhere, vmem, vmem),
            scratch_shapes=[
                pltpu.VMEM((n, rows, cols), jnp.float32),
                pltpu.VMEM((SLOTS, rows, cols), jnp.float32),
                pltpu.VMEM((n, rows, cols), jnp.bfloat16),
                pltpu.VMEM((ns, 2, cols), jnp.float32),
                pltpu.VMEM((ns, max(n - 2, 1), cols), jnp.float32),
                dma((n,)),
                dma((SLOTS,)),
                dma((n,)),
                dma((ns, n)),
                dma((ns - 1, n)),
                dma((ns - 1, n)),
                dma((ns,)),
                dma((ns,)),
                dma((ns,)),
                dma((ns,)),
            ],
            compiler_params=pltpu.CompilerParams(
                collective_id=0, has_side_effects=True, vmem_limit_bytes=62 * 1024 * 1024
            ),
        )(mix_share, w_gate, avg_gate, w_up, avg_up)
        return serve_gate, serve_up, scale_gate, scale_up, serve_router

    return jax.shard_map(
        per_device,
        mesh=mesh,
        in_specs=(
            P("expert", "shard", None),
            P("expert", "shard", None),
            P("expert", "shard", None),
            P("expert", "shard", None),
            P("expert"),
            P("shard", "expert"),
            P("shard"),
        ),
        out_specs=(
            P("expert", None, None),
            P("expert", None, None),
            P("expert", None),
            P("expert", None),
            P(),
        ),
        check_vma=False,
    )
```

time: 1280 us -> 1190 us (0.930)
  waiting for transfers between devices: 1140 us -> 0 us
  Pallas kernels: 0 us -> 1100 us
  other arithmetic: 53.3 us -> 0.01 us
  blocking collectives: 22.4 us -> 40.4 us
  between operations: 13.8 us -> 0.69 us
    pallas_call x0 -> x1, Pallas kernels: none -> 1100 us  [per_device(): pl.pallas_call(functools.partial(kernel, ns, experts, rows), out_shape=(s...]
    all_gather x2 -> x0, waiting for transfers between devices: 1100 us -> none  [the longest x1 562 us: per_device(): lax.all_gather(narrow_up, 'shard', axis=1, tiled=True)]
    psum x1 -> x0, waiting for transfers between devices: 37.2 us -> none  [per_device(): lax.psum((jnp.sum(fresh_gate * fresh_gate, axis=1), jnp.sum(fresh_up * fr...]
    convert_element_type x2 -> x0, other arithmetic: 29.3 us -> none  [the longest x1 29.3 us: per_device(): (fresh_up / jnp.expand_dims(scale_up, 1)).astype(jnp.bfloat16)]
    reduce_sum x1 -> x0, other arithmetic: 23.3 us -> none  [per_device(): jnp.sum(fresh_up * fresh_up, axis=1)]
    all_gather x2 -> x1, blocking collectives: 22.4 us -> 40.4 us  [per_device(): lax.all_gather(part_router, ('shard', 'expert'), axis=0, tiled=False)]
    unnamed x13 -> x12, local copies, waits for them, and re-layouts: 47.2 us -> 47.7 us
  transfers between devices with their start and end apart: 3 -> 0, of which waited for: 3 -> 0; matrix products, arithmetic and copies ran while one was open for 0% -> 0% of each run, Pallas kernels for 0% -> 0%
where the time goes in v1:
time: 1190 us
  Pallas kernels  1100 us (92%)
  local copies, waits for them, and re-layouts  48.4 us (4%)
  blocking collectives  40.4 us (3%)
    pallas_call x1, Pallas kernels, per_device(): pl.pallas_call(functools.partial(kernel, ns, experts, rows), out_shape=(s...  1100 us
    unnamed x12, local copies, waits for them, and re-layouts  47.7 us
    all_gather x1, blocking collectives, per_device(): lax.all_gather(part_router, ('shard', 'expert'), axis=0, tiled=False)  40.4 us

profile of v1, /device:TPU:0, one launch (start us, length us, event | category | flops | bytes accessed | tf_op | source)
XLA Modules:
  0.0 1193.8 jit_solution(6206500560108386424)
XLA Ops:
  0.6 0.0 copy-start.2
  0.6 0.0 copy-start.3
  0.7 1104.3 %shard_map.110 = (bf16[8,2048,1024]{2,1,0:T(8,128)(2,1)}, bf16[8,2048,1024]{2,1,0:T(8,128)(2,1)}, f32[8,1024]{1,0:T(8,128)}, f32[8,1024]{1,0:T(8,128)}) custom-call(f32[8]{0:T(128)} %mix_ref.1, f32[8,512,1024]{2,1,0:T(8,128)} %wg_ref.1, f32[8,512,1024]{2,1,0:T(8,128)} %ag_ref.1, f32[8,512,1024]{2,1,0:T(8,128)} %wu_ref.1, f32[8,512,1024]{2,1,0:T(8,128)} %au_ref.1), custom_call_target="tpu_custom_call" | custom-call | tf_op jit(solution)/shard_map/pallas_call | solution.py:231
  1104.9 0.0 copy-done.2
  1104.9 0.0 copy-done.3
  1105.0 40.4 %all-gather = bf16[256,512]{1,0:T(8,128)(2,1)S(1)} all-gather(bf16[8,512]{1,0:T(8,128)(2,1)S(1)} %fusion), channel_id=2, replica_groups=mesh['expert'=8,'shard'=4] {'shard','expert'}, dimensions={0}, use_global_device_ids=true | all-gather | bytes 270336 | tf_op jit(solution)/shard_map/all_gather | solution.py:227
  1145.4 0.7 copy.12
  1146.1 23.2 %copy.17 = bf16[8,2048,1024]{2,1,0:T(8,128)(2,1)} copy(bf16[8,2048,1024]{2,1,0:T(8,128)(2,1)} %get-tuple-element.18) | data formatting | bytes 67108864
  1169.3 0.0 copy-start.1
  1169.3 0.0 copy-start
  1169.3 23.2 %copy.18 = bf16[8,2048,1024]{2,1,0:T(8,128)(2,1)} copy(bf16[8,2048,1024]{2,1,0:T(8,128)(2,1)} %get-tuple-element.19) | data formatting | bytes 67108864
  1192.6 0.0 copy-done.1
  1192.6 0.6 copy.19
  1193.2 0.0 copy-done
  1193.2 0.6 copy.20
  (1 shorter events, 0.0 us)
Async XLA Ops:
  0.6 1104.3 %copy-start.2 = (f32[512,8]{0,1:T(8,128)S(1)}, f32[512,8]{0,1:T(8,128)}, u32[]{:S(2)}) copy-start(f32[512,8]{0,1:T(8,128)} %param.12) | copy-start | bytes 49156
  0.6 1104.3 %copy-start.3 = (f32[512]{0:T(512)S(1)}, f32[512]{0:T(512)}, u32[]{:S(2)}) copy-start(f32[512]{0:T(512)} %param.13) | copy-start | bytes 6148
  1169.3 23.3 %copy-start.1 = (f32[8,1024]{1,0:T(8,128)S(1)}, f32[8,1024]{1,0:T(8,128)}, u32[]{:S(2)}) copy-start(f32[8,1024]{1,0:T(8,128)} %get-tuple-element.20) | copy-start | bytes 98308
  1169.3 23.9 %copy-start = (f32[8,1024]{1,0:T(8,128)S(1)}, f32[8,1024]{1,0:T(8,128)}, u32[]{:S(2)}) copy-start(f32[8,1024]{1,0:T(8,128)} %get-tuple-element.21) | copy-start | bytes 98308
